TPU v7x, 32 devices: a whole 2x2x4 slice. The times are simulated.
32 devices in a mesh: fsdp: 4 (over y, x), ctx: 4 (over z), tp: 2 (over core).
Axes of the slice: x: 2, y: 2, z: 4, core: 2. Of those that a mesh axis runs over, the one named last changes fastest.
Arguments:
- tokens: bfloat16 [8, 1024, 768], P('fsdp', 'ctx'), may hold values from -6 to 6
- lengths: int32 [8], P('fsdp'), may hold values from 256 to 1024, as said below
- cotangent: bfloat16 [8, 1024, 768], P('fsdp', 'ctx'), may hold values from -6 to 6
- ln1_gain: float32 [768], replicated, may hold values from 0.5 to 1.5
- ln1_bias: float32 [768], replicated, may hold values from -1.8 to 1.8
- qkv_weight: bfloat16 [768, 3, 768], P('fsdp', None, 'tp'), may hold values from -0.21875 to 0.21875
- conv_kernel: float32 [3, 3, 768], P(None, None, 'tp'), may hold values from -3.5 to 3.5
- conv_bias: float32 [3, 768], P(None, 'tp'), may hold values from -1.8 to 1.8
- out_weight: bfloat16 [768, 768], P('tp', 'fsdp'), may hold values from -1.75 to 1.75
- ln2_gain: float32 [768], replicated, may hold values from 0.5 to 1.5
- ln2_bias: float32 [768], replicated, may hold values from -1.8 to 1.8
- up_weight: bfloat16 [768, 3072], P('fsdp', 'tp'), may hold values from -0.21875 to 0.21875
- down_weight: bfloat16 [3072, 768], P('tp', 'fsdp'), may hold values from -0.109375 to 0.109375
Outputs:
- result: bfloat16 [8, 1024, 768], P('fsdp', 'ctx')
- input_grad: float32 [8, 1024, 768], P('fsdp', 'ctx')
- ln1_gain_grad: float32 [768], replicated
- ln1_bias_grad: float32 [768], replicated
- qkv_weight_grad: float32 [768, 3, 768], P('fsdp', None, 'tp')
- conv_kernel_grad: float32 [3, 3, 768], P(None, None, 'tp')
- conv_bias_grad: float32 [3, 768], P(None, 'tp')
- out_weight_grad: float32 [768, 768], P('tp', 'fsdp')
- ln2_gain_grad: float32 [768], replicated
- ln2_bias_grad: float32 [768], replicated
- up_weight_grad: float32 [768, 3072], P('fsdp', 'tp')
- down_weight_grad: float32 [3072, 768], P('tp', 'fsdp')
Inputs may be any that keep to these rules, and one draw needn't show every extreme that they name: `lengths`: some slot holds 1024 tokens and some other slot 256.
All inputs are finite; a program needn't handle non-finite values.
Results may differ from a plain program's by a relative error of at most 0.014.
The roundings to bfloat16 on the way count: a program that leaves them out, or rounds other values in their place, can miss the bound.
Values may be sent and summed in bfloat16 or wider, within the bound.
A program may use at most 256 MiB of HBM per device.

v0:
```python
import jax
import jax.numpy as jnp
from jax import lax
from jax.sharding import PartitionSpec as P

HD = 64
EPSILON = 1e-05
SCALING = 0.125
MASKED = -1e30


def shifted(block, axis, distance):
    devices = range(lax.axis_size(axis))
    route = [(i - distance, i) for i in devices if i - distance in devices]
    return lax.ppermute(block, axis, route)


def layer_norm(row_data, norm_gain, shift_bias):
    centred = row_data - jnp.mean(row_data, axis=-1, keepdims=True)
    recip = lax.rsqrt(jnp.mean(centred * centred, axis=-1, keepdims=True) + EPSILON)
    normed = centred * recip
    return (normed * norm_gain + shift_bias, normed, recip)


def norm_back(grad_in, normed, recip, norm_gain):
    scaled = grad_in * norm_gain
    return recip * (
        scaled
        - jnp.mean(scaled, axis=-1, keepdims=True)
        - normed * jnp.mean(scaled * normed, axis=-1, keepdims=True)
    )


def tile_scores(query_part, key_part, query_pos, key_pos, lengths):
    scores = (
        jnp.einsum("mqhd,mkhd->mhqk", query_part, key_part, preferred_element_type=jnp.float32)
        * SCALING
    )
    allowed = (key_pos[None, None, :] <= query_pos[None, :, None]) & (
        key_pos[None, None, :] < lengths[:, None, None]
    )
    return jnp.where(allowed[:, None], scores, MASKED)


def tile_grads(
    query_part, key_part, value_part, grad_part, log_part, delta_part, query_pos, key_pos, lengths
):
    probs_full = jnp.exp(tile_scores(query_part, key_part, query_pos, key_pos, lengths) - log_part)
    prob_grad = jnp.einsum(
        "mqhd,mkhd->mhqk", grad_part, value_part, preferred_element_type=jnp.float32
    )
    score_grad = (probs_full * (prob_grad - delta_part)).astype(jnp.bfloat16)
    return (probs_full, prob_grad, score_grad)


def local(
    tokens,
    lengths,
    cotangent,
    ln1_gain,
    ln1_bias,
    qkv_weight,
    conv_kernel,
    conv_bias,
    out_weight,
    ln2_gain,
    ln2_bias,
    up_weight,
    down_weight,
):
    batches, block_rows, model_width = tokens.shape
    all_rows = batches * block_rows
    qkv_full, out_full, up_full_w, down_full_w = (
        lax.all_gather(qkv_weight, "fsdp", axis=0, tiled=True),
        lax.all_gather(out_weight, "fsdp", axis=1, tiled=True),
        lax.all_gather(up_weight, "fsdp", axis=0, tiled=True),
        lax.all_gather(down_weight, "fsdp", axis=1, tiled=True),
    )
    local_width = qkv_full.shape[2]
    local_heads = local_width // HD
    ctx_count = lax.axis_size("ctx")
    slot_span = block_rows * ctx_count
    group_blocks = 4
    key_span = block_rows * group_blocks
    ctx_index = lax.axis_index("ctx")
    positions = ctx_index * block_rows + jnp.arange(block_rows, dtype=jnp.int32)
    span_iota = jnp.arange(key_span, dtype=jnp.int32)
    block_count = (ctx_index * block_rows + block_rows + key_span - 1) // key_span
    token_valid = positions[None, :] < lengths[:, None]

    def span_slice(array_data, block, axis_pos):
        return lax.dynamic_slice_in_dim(array_data, block * key_span, key_span, axis_pos)

    inputs = tokens.astype(jnp.float32).reshape(all_rows, model_width)
    first_out, first_hat, first_recip = layer_norm(inputs, ln1_gain, ln1_bias)
    first_low = first_out.astype(jnp.bfloat16)
    pre_low = jnp.einsum(
        "td,dcn->tcn", first_low, qkv_full, preferred_element_type=jnp.float32
    ).astype(jnp.bfloat16)
    pre_low = pre_low.reshape(batches, block_rows, 3, local_width)
    earlier = shifted(pre_low[:, block_rows - 2 :], "ctx", 1)
    extended = jnp.concatenate([earlier, pre_low], axis=1).astype(jnp.float32)
    conv_out = (
        conv_bias
        + conv_kernel[0] * extended[:, 2:]
        + conv_kernel[1] * extended[:, 1:-1]
        + conv_kernel[2] * extended[:, :-2]
    ).astype(jnp.bfloat16)
    query_heads = conv_out[:, :, 0].reshape(batches, block_rows, local_heads, HD)
    own_pairs = conv_out[:, :, 1:]
    whole_pairs = lax.all_gather(own_pairs, "ctx", axis=1, tiled=True)
    key_heads = whole_pairs[:, :, 0].reshape(batches, slot_span, local_heads, HD)
    value_heads = whole_pairs[:, :, 1].reshape(batches, slot_span, local_heads, HD)

    def stat_step(block, carry):
        row_max, total = carry
        key_pos = block * key_span + span_iota
        scores = tile_scores(
            query_heads, span_slice(key_heads, block, 1), positions, key_pos, lengths
        )
        new_max = jnp.maximum(row_max, jnp.max(scores, axis=-1, keepdims=True))
        total = total * jnp.exp(row_max - new_max) + jnp.sum(
            jnp.exp(scores - new_max), axis=-1, keepdims=True
        )
        return (new_max, total)

    stat_shape = (batches, local_heads, block_rows, 1)
    row_max, total = lax.fori_loop(
        0,
        block_count,
        stat_step,
        (jnp.full(stat_shape, MASKED, jnp.float32), jnp.zeros(stat_shape, jnp.float32)),
    )
    log_total = row_max + jnp.log(total)

    def value_step(block, accum):
        key_pos = block * key_span + span_iota
        scores = tile_scores(
            query_heads, span_slice(key_heads, block, 1), positions, key_pos, lengths
        )
        probs_low = jnp.exp(scores - log_total).astype(jnp.bfloat16)
        return accum + jnp.einsum(
            "mhqk,mkhd->mqhd",
            probs_low,
            span_slice(value_heads, block, 1),
            preferred_element_type=jnp.float32,
        )

    attn_acc = lax.fori_loop(
        0, block_count, value_step, jnp.zeros((batches, block_rows, local_heads, HD), jnp.float32)
    )
    attn_low = attn_acc.reshape(all_rows, local_width).astype(jnp.bfloat16)
    attn_out = lax.psum(jnp.dot(attn_low, out_full, preferred_element_type=jnp.float32), "tp")
    middle = inputs + attn_out
    second_out, second_hat, second_recip = layer_norm(middle, ln2_gain, ln2_bias)
    second_low = second_out.astype(jnp.bfloat16)
    up_full = jnp.dot(second_low, up_full_w, preferred_element_type=jnp.float32)
    rectified = jnp.maximum(up_full, 0.0)
    act_low = (rectified * rectified).astype(jnp.bfloat16)
    ffn_out = lax.psum(jnp.dot(act_low, down_full_w, preferred_element_type=jnp.float32), "tp")
    result = (middle + ffn_out).reshape(batches, block_rows, model_width).astype(jnp.bfloat16)
    grad_out = (
        cotangent.astype(jnp.float32) * token_valid[:, :, None].astype(jnp.float32)
    ).reshape(all_rows, model_width)
    grad_low = grad_out.astype(jnp.bfloat16)
    down_wgrad = jnp.einsum("tf,td->fd", act_low, grad_low, preferred_element_type=jnp.float32)
    act_grad = jnp.einsum("td,fd->tf", grad_low, down_full_w, preferred_element_type=jnp.float32)
    up_grad_low = (act_grad * 2.0 * rectified).astype(jnp.bfloat16)
    up_wgrad = jnp.einsum("td,tf->df", second_low, up_grad_low, preferred_element_type=jnp.float32)
    second_grad = lax.psum(
        jnp.einsum("tf,df->td", up_grad_low, up_full_w, preferred_element_type=jnp.float32), "tp"
    )
    gain_two_grad = jnp.sum(second_grad * second_hat, axis=0)
    bias_two_grad = jnp.sum(second_grad, axis=0)
    middle_grad = grad_out + norm_back(second_grad, second_hat, second_recip, ln2_gain)
    middle_low = middle_grad.astype(jnp.bfloat16)
    out_wgrad = jnp.einsum("tn,td->nd", attn_low, middle_low, preferred_element_type=jnp.float32)
    attn_flat = jnp.einsum(
        "td,nd->tn", middle_low, out_full, preferred_element_type=jnp.float32
    ).astype(jnp.bfloat16)
    attn_grad = attn_flat.reshape(batches, block_rows, local_heads, HD)

    def delta_step(block, accum):
        key_pos = block * key_span + span_iota
        probs_full = jnp.exp(
            tile_scores(query_heads, span_slice(key_heads, block, 1), positions, key_pos, lengths)
            - log_total
        )
        prob_grad = jnp.einsum(
            "mqhd,mkhd->mhqk",
            attn_grad,
            span_slice(value_heads, block, 1),
            preferred_element_type=jnp.float32,
        )
        return accum + jnp.sum(probs_full * prob_grad, axis=-1, keepdims=True)

    delta = lax.fori_loop(0, block_count, delta_step, jnp.zeros(stat_shape, jnp.float32))
    query_zero = jnp.zeros((batches, block_rows, local_heads, HD), jnp.float32)

    def back_step(block, carry):
        accum, buffer = carry
        key_pos = block * key_span + span_iota
        key_part = span_slice(key_heads, block, 1)
        probs_full, prob_grad, score_grad = tile_grads(
            query_heads,
            key_part,
            span_slice(value_heads, block, 1),
            attn_grad,
            log_total,
            delta,
            positions,
            key_pos,
            lengths,
        )
        probs_again = probs_full.astype(jnp.bfloat16)
        accum = (
            accum
            + jnp.einsum(
                "mhqk,mkhd->mqhd", score_grad, key_part, preferred_element_type=jnp.float32
            )
            * SCALING
        )
        key_term = (
            jnp.einsum(
                "mhqk,mqhd->mkhd", score_grad, query_heads, preferred_element_type=jnp.float32
            )
            * SCALING
        )
        value_term = jnp.einsum(
            "mhqk,mqhd->mkhd", probs_again, attn_grad, preferred_element_type=jnp.float32
        )
        stacked = jnp.stack(
            [
                key_term.reshape(batches, key_span, local_width),
                value_term.reshape(batches, key_span, local_width),
            ],
            axis=2,
        )
        buffer = lax.dynamic_update_slice_in_dim(buffer, stacked, block * key_span, 1)
        return (accum, buffer)

    buffer_zero = jnp.zeros((batches, slot_span, 2, local_width), jnp.float32)
    query_grad, pair_terms = lax.fori_loop(0, block_count, back_step, (query_zero, buffer_zero))
    pair_grad = lax.psum_scatter(pair_terms, "ctx", scatter_dimension=1, tiled=True)
    mixed_grad = jnp.concatenate(
        [query_grad.reshape(batches, block_rows, 1, local_width), pair_grad], axis=2
    )
    later = shifted(mixed_grad[:, :2], "ctx", -1)
    ahead = jnp.concatenate([mixed_grad, later], axis=1)
    pre_grad = (
        conv_kernel[0] * ahead[:, :block_rows]
        + conv_kernel[1] * ahead[:, 1 : block_rows + 1]
        + conv_kernel[2] * ahead[:, 2:]
    ).astype(jnp.bfloat16)
    kernel_grad = jnp.stack(
        [
            jnp.sum(extended[:, 2 - offset : 2 - offset + block_rows] * mixed_grad, axis=(0, 1))
            for offset in range(3)
        ]
    )
    shift_grad = jnp.sum(mixed_grad, axis=(0, 1))
    pre_grad = pre_grad.reshape(all_rows, 3, local_width)
    qkv_wgrad = jnp.einsum("td,tcn->dcn", first_low, pre_grad, preferred_element_type=jnp.float32)
    first_grad = lax.psum(
        jnp.einsum("tcn,dcn->td", pre_grad, qkv_full, preferred_element_type=jnp.float32), "tp"
    )
    gain_one_grad = jnp.sum(first_grad * first_hat, axis=0)
    bias_one_grad = jnp.sum(first_grad, axis=0)
    input_grad = middle_grad + norm_back(first_grad, first_hat, first_recip, ln1_gain)
    input_grad = input_grad.reshape(batches, block_rows, model_width)

    def owned(term, axis_pos):
        part = lax.psum_scatter(
            term.astype(jnp.bfloat16), "fsdp", scatter_dimension=axis_pos, tiled=True
        )
        return lax.psum(part, "ctx").astype(jnp.float32)

    qkv_share = owned(qkv_wgrad, 0)
    out_share = owned(out_wgrad, 1)
    up_share = owned(up_wgrad, 0)
    down_share = owned(down_wgrad, 1)
    small_sums = lax.psum(
        (gain_one_grad, bias_one_grad, kernel_grad, shift_grad, gain_two_grad, bias_two_grad),
        ("fsdp", "ctx"),
    )
    return (
        result,
        input_grad,
        small_sums[0],
        small_sums[1],
        qkv_share,
        small_sums[2],
        small_sums[3],
        out_share,
        small_sums[4],
        small_sums[5],
        up_share,
        down_share,
    )


def solution(mesh):
    placed = (
        P("fsdp", "ctx", None),
        P("fsdp"),
        P("fsdp", "ctx", None),
        P(),
        P(),
        P("fsdp", None, "tp"),
        P(None, None, "tp"),
        P(None, "tp"),
        P("tp", "fsdp"),
        P(),
        P(),
        P("fsdp", "tp"),
        P("tp", "fsdp"),
    )
    return jax.shard_map(
        local,
        mesh=mesh,
        in_specs=placed,
        out_specs=(
            P("fsdp", "ctx", None),
            P("fsdp", "ctx", None),
            P(),
            P(),
            P("fsdp", None, "tp"),
            P(None, None, "tp"),
            P(None, "tp"),
            P("tp", "fsdp"),
            P(),
            P(),
            P("fsdp", "tp"),
            P("tp", "fsdp"),
        ),
        check_vma=False,
    )
```

profile of v0, /device:TPU:0, one launch (start us, length us, event | category | flops | bytes accessed | tf_op | source)
XLA Modules:
  0.0 692.8 jit_solution(6675761201139919809)
XLA Ops:
  10.7 34.4 %all-gather.5.cloned.1.call-done = bf16[768,3,384]{2,0,1:T(8,128)(2,1)} async-done(((bf16[192,3,384]{2,0,1:T(8,128)(2,1)}), bf16[768,3,384]{2,0,1:T(8,128)(2,1)}) %all-gather.5.cloned.1.call-update) | async-done | bytes 1769488 | tf_op jit(solution)/shard_map/all_gather | solution.py:74
  45.1 2.7 convolution_convert_fusion.2
  47.8 3.4 collective-permute-start
  53.8 2.1 add_convert_fusion
  56.9 11.0 %all_gather.17 = bf16[384,768]{0,1:T(8,128)(2,1)S(1)} all-gather(bf16[384,192]{0,1:T(8,128)(2,1)S(1)} %copy-done.29), channel_id=1, replica_groups=mesh['fsdp'=4,'ctx'=4,'tp'=2] {'fsdp'}, dimensions={1}, use_global_device_ids=true | all-gather | bytes 737280 | tf_op jit(solution)/shard_map/all_gather | solution.py:75
  68.0 53.2 %all-gather.7.cloned.1.call-done = bf16[2,1024,2,384]{1,3,0,2:T(8,128)(2,1)} async-done(((bf16[2,256,2,384]{1,3,0,2:T(8,128)(2,1)}), bf16[2,1024,2,384]{1,3,0,2:T(8,128)(2,1)}) %all-gather.7.cloned.1.call-update) | async-done | bytes 3145744 | tf_op jit(solution)/shard_map/all_gather | solution.py:111
  121.2 3.5 fusion.71
  124.7 6.7 while.48
  125.3 2.4 fusion.137
  127.7 3.6 exponential_reduce_fusion.2
  132.3 8.3 %while.49 = (s32[]{:T(128)}, f32[2,256,6,64]{1,3,2,0:T(8,128)}, s32[]{:T(128)}, s32[2]{0:T(128)S(1)}, bf16[2,256,6,64]{1,3,2,0:T(8,128)(2,1)S(1)}, /*index=5*/bf...) while((s32[]{:T(128)}, f32[2,256,6,64]{1,3,2,0:T(8,128)}, ...), condition=%wide.region_7.8_spmd.clone, body=%wide.region_6.7_spmd.clone.sunk | while | flops 818875648 | bytes 6715529 | solution.py:149
  133.1 7.6 %fusion.141 = f32[2,256,6,64]{1,3,2,0:T(8,128)} fusion(f32[2,256,6,64]{1,3,2,0:T(8,128)} %get-tuple-element.885, bf16[2,1024,6,64]{1,3,2,0:T(8,128)(2,1)} %get-tuple-element.902, f32[2,6,256]{2,1,0:T(8,128)S(1)} %bitcast.217, pred[2,256,1024]{2,1,0:T(8,128)(4,1)S(1)} %broadcast_and_fusion.9, bf16[2,256,6,64]{1,3,2,0:T(8,128)(2,1)S(1)} %get-tuple-element.899, ...), kind=kOutput, calls=%fused_computation.23.clone.1 | convolution fusion | flops 818085888 | bytes 5648384 | tf_op jit(solution)/shard_map/while/body/mhqk,mkhd->mqhd/dot_general | solution.py:142
  142.3 1.8 fusion.74
  147.8 15.0 %all-reduce.8.cloned.1.call-done = f32[512,768]{1,0:T(8,128)} async-done(((f32[512,768]{1,0:T(8,128)}), f32[512,768]{1,0:T(8,128)}) %all-reduce.8.cloned.1.call-update) | async-done | bytes 1572880 | tf_op jit(solution)/shard_map/psum | solution.py:153
  162.9 1.8 fusion.70
  165.1 38.1 %all-gather.9.cloned.1.call-done = bf16[768,1536]{1,0:T(8,128)(2,1)} async-done(((bf16[192,1536]{1,0:T(8,128)(2,1)}), bf16[768,1536]{1,0:T(8,128)(2,1)}) %all-gather.9.cloned.1.call-update) | async-done | bytes 2359312 | tf_op jit(solution)/shard_map/all_gather | solution.py:76
  203.1 4.9 convolution_maximum_fusion
  208.0 34.1 %all-gather.11.cloned.1.call-done = bf16[1536,768]{0,1:T(8,128)(2,1)} async-done(((bf16[1536,192]{0,1:T(8,128)(2,1)}), bf16[1536,768]{0,1:T(8,128)(2,1)}) %all-gather.11.cloned.1.call-update) | async-done | bytes 2359312 | tf_op jit(solution)/shard_map/all_gather | solution.py:77
  242.2 4.4 fusion.34
  247.8 2.6 fusion.75
  250.7 20.2 %all-reduce.10.cloned.1.call-done = f32[512,768]{1,0:T(8,128)} async-done(((f32[512,768]{1,0:T(8,128)}), f32[512,768]{1,0:T(8,128)}) %all-reduce.10.cloned.1.call-update) | async-done | bytes 1572880 | tf_op jit(solution)/shard_map/psum | solution.py:170
  271.0 2.9 multiply_reduce_fusion.4
  276.9 7.2 %while.50 = (s32[]{:T(128)}, f32[2,6,256,1]{2,0,1,3:T(2,128)S(1)}, s32[]{:T(128)}, s32[2]{0:T(128)S(1)}, bf16[2,256,6,64]{1,3,2,0:T(8,128)(2,1)S(1)}, /*index=5*...) while((s32[]{:T(128)}, f32[2,6,256,1]{2,0,1,3:T(2,128)S(1)}, ...), condition=%wide.region_17.18_spmd.clone, body=%wide.region_15.17_spmd.clone.sunk | while | flops 821824768 | bytes 37042348 | solution.py:197
  279.3 4.7 multiply_reduce_fusion.10
  284.9 3.4 broadcast_in_dim.65
  288.4 19.2 %while.51 = (s32[]{:T(128)}, f32[2,256,6,64]{1,3,2,0:T(8,128)S(1)}, f32[2,1024,2,384]{1,3,0,2:T(8,128)}, s32[]{:T(128)}, s32[2]{0:T(128)S(1)}, /*index=5*/bf16[2...) while((s32[]{:T(128)}, f32[2,256,6,64]{1,3,2,0:T(8,128)S(1)}, ...), condition=%wide.region_19.20_spmd.clone, body=%wide.region_18.19_spmd.clone.sunk | while | flops 2048265472 | bytes 87087288 | solution.py:243
  291.2 3.4 fusion.159
  294.6 6.5 multiply_convert_fusion.5
  301.1 2.1 fusion.158
  304.4 3.2 pad_maximum_fusion.5
  310.6 4.9 convolution_convert_fusion
  317.2 4.4 convolution_convert_fusion.1
  321.7 98.0 %reduce-scatter.6.cloned.1.call-done = f32[2,256,2,384]{1,3,0,2:T(8,128)} async-done(((f32[2,1024,2,384]{1,3,0,2:T(8,128)}), f32[2,256,2,384]{1,3,0,2:T(8,128)}) %reduce-scatter.6.cloned.1.call-update) | async-done | bytes 1572880 | tf_op jit(solution)/shard_map/reduce_scatter | solution.py:244
  419.7 2.2 fusion.56
  424.9 4.4 collective-permute-done.1
  430.7 2.2 pad_maximum_fusion.1
  434.0 4.5 multiply_reduce_fusion.3
  439.5 2.7 bitcast_convert_fusion
  442.3 5.4 fusion.65
  449.1 4.2 convolution_bitcast_fusion
  453.5 36.1 %reduce-scatter.14.cloned.1.call-done = bf16[1536,192]{0,1:T(8,128)(2,1)} async-done(((bf16[1536,768]{0,1:T(8,128)(2,1)}), bf16[1536,192]{0,1:T(8,128)(2,1)}) %reduce-scatter.14.cloned.1.call-update) | async-done | bytes 589840 | tf_op jit(solution)/shard_map/reduce_scatter | solution.py:273
  489.6 40.3 %reduce-scatter.12.cloned.1.call-done = bf16[192,1536]{1,0:T(8,128)(2,1)} async-done(((bf16[768,1536]{1,0:T(8,128)(2,1)}), bf16[192,1536]{1,0:T(8,128)(2,1)}) %reduce-scatter.12.cloned.1.call-update) | async-done | bytes 589840 | tf_op jit(solution)/shard_map/reduce_scatter | solution.py:273
  529.9 35.6 %reduce-scatter.8.cloned.1.call-done = bf16[192,3,384]{2,0,1:T(8,128)(2,1)} async-done(((bf16[768,3,384]{2,0,1:T(8,128)(2,1)}), bf16[192,3,384]{2,0,1:T(8,128)(2,1)}) %reduce-scatter.8.cloned.1.call-update) | async-done | bytes 442384 | tf_op jit(solution)/shard_map/reduce_scatter | solution.py:273
  565.5 26.1 %all-reduce.12.cloned.1.call-done = (f32[512,768]{1,0:T(8,128)}, f32[512,768]{1,0:T(8,128)}) async-done(((f32[512,768]{1,0:T(8,128)}, f32[512,768]{1,0:T(8,128)}), (f32[512,768]{1,0:T(8,128)}, f32[512,768]{1,0:T(8,128)})) %all-reduce.12.cloned.1.call-update) | async-done | bytes 3145744 | tf_op jit(solution)/shard_map/psum | solution.py:160
  591.6 2.2 fusion.55
  593.8 81.9 %all-reduce = (f32[768]{0:T(1024)}, f32[768]{0:T(1024)}, f32[3,3,384]{2,1,0:T(4,128)}, f32[3,384]{1,0:T(4,128)}, f32[768]{0:T(1024)}, /*index=5*/f32[768]{0:T(1024)}) all-reduce(f32[768]{0:T(1024)S(1)} %get-tuple-element.486, f32[768]{0:T(1024)S(1)} %get-tuple-element.492, ...), channel_id=1, replica_groups=mesh['fsdp'=4,'ctx'=4,'tp'=2] {'fsdp','ctx'}, use_global_device_ids=true, to_apply=%region_25.26 | all-reduce | flops 7680 | bytes 61440 | tf_op jit(solution)/shard_map/psum | solution.py:282
  675.7 2.6 add_convert_fusion.1
  681.8 2.0 convert_element_type.115
  (237 shorter events, 44.5 us)
Async XLA Ops:
  7.2 3.1 copy-start.36
  7.2 37.9 %all-gather.5.cloned.1.call-start = ((), (), s32[]{:S(2)}) async-start(), calls=%async_computation.5 | async-start | bytes 2211840 | tf_op jit(solution)/shard_map/all_gather | solution.py:74
  7.9 113.2 %all-gather.7.cloned.1.call-start = ((), (), s32[]{:S(2)}) async-start(), calls=%async_computation.6 | async-start | bytes 3932160 | tf_op jit(solution)/shard_map/all_gather | solution.py:111
  9.3 38.4 %copy-start.38 = (f32[1,2,2,128]{3,1,2,0:T(2,128)}, f32[1,2,2,128]{3,1,2,0:T(2,128)S(1)}, u32[]{:S(2)}) copy-start(f32[1,2,2,128]{3,1,2,0:T(2,128)S(1)} %copy.100) | copy-start | bytes 6148
  10.3 37.4 %copy-start.40 = (f32[1,2,2,128]{3,1,2,0:T(2,128)}, f32[1,2,2,128]{3,1,2,0:T(2,128)S(1)}, u32[]{:S(2)}) copy-start(f32[1,2,2,128]{3,1,2,0:T(2,128)S(1)} %copy.101) | copy-start | bytes 6148
  10.7 40.5 %copy-start.49 = (f32[3,3,384]{2,1,0:T(4,128)S(1)}, f32[3,3,384]{2,1,0:T(4,128)}, u32[]{:S(2)}) copy-start(f32[3,3,384]{2,1,0:T(4,128)} %param.27) | copy-start | bytes 41476
  47.8 4.8 collective-permute-start
  55.9 12.1 %copy-start = (bf16[2,256,3,384]{1,3,0,2:T(8,128)(2,1)}, bf16[2,256,3,384]{1,3,0,2:T(8,128)(2,1)S(1)}, u32[]{:S(2)}) copy-start(bf16[2,256,3,384]{1,3,0,2:T(8,128)(2,1)S(1)} %add_convert_fusion) | copy-start | bytes 3538948
  56.8 106.0 %all-reduce.8.cloned.1.call-start = ((), (), s32[]{:S(2)}) async-start(), calls=%async_computation.7 | async-start | bytes 3145728 | tf_op jit(solution)/shard_map/psum | solution.py:153
  68.0 74.3 %copy-start.15 = (bf16[384,768]{0,1:T(8,128)(2,1)}, bf16[384,768]{0,1:T(8,128)(2,1)S(1)}, u32[]{:S(2)}) copy-start(bf16[384,768]{0,1:T(8,128)(2,1)S(1)} %all_gather.17) | copy-start | bytes 1769476
  68.0 56.7 %slice-start = ((bf16[2,256,3,384]{1,3,0,2:T(8,128)(2,1)}), bf16[2,256,1,384]{1,3,0,2:T(8,128)(2,1)S(1)}, s32[]{:S(2)}) async-start(bf16[2,256,3,384]{1,3,0,2:T(8,128)(2,1)} %copy-done), calls=%async_computation.18 | async-start | bytes 786432 | tf_op jit(solution)/shard_map/slice | solution.py:109
  68.0 56.7 %copy-start.28 = (s32[2]{0:T(128)S(1)}, s32[2]{0:T(128)}, u32[]{:S(2)}) copy-start(s32[2]{0:T(128)} %param.22) | copy-start | bytes 28
  140.6 3.5 copy-start.52
  144.2 59.0 %all-gather.9.cloned.1.call-start = ((), (), s32[]{:S(2)}) async-start(), calls=%async_computation.8 | async-start | bytes 2949120 | tf_op jit(solution)/shard_map/all_gather | solution.py:76
  144.8 97.4 %all-gather.11.cloned.1.call-start = ((), (), s32[]{:S(2)}) async-start(), calls=%async_computation.9 | async-start | bytes 2949120 | tf_op jit(solution)/shard_map/all_gather | solution.py:77
  145.3 125.6 %all-reduce.10.cloned.1.call-start = ((), (), s32[]{:S(2)}) async-start(), calls=%async_computation.10 | async-start | bytes 3145728 | tf_op jit(solution)/shard_map/psum | solution.py:170
  164.7 109.1 %copy-start.3 = (f32[512,768]{1,0:T(8,128)}, f32[512,768]{1,0:T(8,128)S(1)}, u32[]{:S(2)}) copy-start(f32[512,768]{1,0:T(8,128)S(1)} %get-tuple-element.584) | copy-start | bytes 4718596
  164.7 38.4 %copy-start.54 = (f32[768]{0:T(1024)S(1)}, f32[768]{0:T(1024)}, u32[]{:S(2)}) copy-start(f32[768]{0:T(1024)} %param.30) | copy-start | bytes 9220
  164.7 109.1 %copy-start.42 = (f32[512]{0:T(512)}, f32[512]{0:T(512)S(1)}, u32[]{:S(2)}) copy-start(f32[512]{0:T(512)S(1)} %broadcast_multiply_fusion.4) | copy-start | bytes 6148
  165.1 108.8 %copy-start.47 = (f32[512]{0:T(512)}, f32[512]{0:T(512)S(1)}, u32[]{:S(2)}) copy-start(f32[512]{0:T(512)S(1)} %add_rsqrt_fusion) | copy-start | bytes 6148
  242.2 5.6 copy-start.62
  250.5 169.3 %reduce-scatter.6.cloned.1.call-start = ((), (), s32[]{:S(2)}) async-start(), calls=%async_computation.11 | async-start | bytes 7864320 | tf_op jit(solution)/shard_map/reduce_scatter | solution.py:244
  307.6 145.8 %reduce-scatter.10.cloned.1.call-start = ((), (), s32[]{:S(2)}) async-start(), calls=%async_computation.13 | async-start | bytes 737280 | tf_op jit(solution)/shard_map/reduce_scatter | solution.py:273
  310.5 179.0 %reduce-scatter.14.cloned.1.call-start = ((), (), s32[]{:S(2)}) async-start(), calls=%async_computation.15 | async-start | bytes 2949120 | tf_op jit(solution)/shard_map/reduce_scatter | solution.py:273
  315.5 214.4 %reduce-scatter.12.cloned.1.call-start = ((), (), s32[]{:S(2)}) async-start(), calls=%async_computation.14 | async-start | bytes 2949120 | tf_op jit(solution)/shard_map/reduce_scatter | solution.py:273
  321.7 243.7 %reduce-scatter.8.cloned.1.call-start = ((), (), s32[]{:S(2)}) async-start(), calls=%async_computation.12 | async-start | bytes 2211840 | tf_op jit(solution)/shard_map/reduce_scatter | solution.py:273
  423.6 5.7 collective-permute-start.1
  430.7 3.3 copy-start.10
  430.7 3.3 copy-start.31
  430.7 3.3 copy-start.33
  430.7 3.3 copy-start.35
  434.0 5.5 copy-start.6
  434.0 5.5 copy-start.37
  434.0 5.5 copy-start.57
  434.0 5.5 copy-start.60
  434.0 5.5 copy-start.61
  442.3 5.4 copy-start.18
  442.3 149.3 %all-reduce.12.cloned.1.call-start = ((), (), s32[]{:S(2)}) async-start(), calls=%async_computation.16 | async-start | bytes 6291456 | tf_op jit(solution)/shard_map/psum | solution.py:160
  453.4 112.1 %copy-start.44 = (f32[3,384]{1,0:T(4,128)S(1)}, f32[3,384]{1,0:T(4,128)}, u32[]{:S(2)}) copy-start(f32[3,384]{1,0:T(4,128)} %get-tuple-element.481) | copy-start | bytes 13828
  453.4 112.1 %copy-start.45 = (f32[3,384]{1,0:T(4,128)S(1)}, f32[3,384]{1,0:T(4,128)}, u32[]{:S(2)}) copy-start(f32[3,384]{1,0:T(4,128)} %get-tuple-element.482) | copy-start | bytes 13828
  453.4 112.1 %copy-start.46 = (f32[3,384]{1,0:T(4,128)S(1)}, f32[3,384]{1,0:T(4,128)}, u32[]{:S(2)}) copy-start(f32[3,384]{1,0:T(4,128)} %get-tuple-element.483) | copy-start | bytes 13828
  453.4 138.2 %copy-start.39 = (f32[1,2,2,128]{3,1,2,0:T(2,128)S(1)}, f32[1,2,2,128]{3,1,2,0:T(2,128)}, u32[]{:S(2)}) copy-start(f32[1,2,2,128]{3,1,2,0:T(2,128)} %copy-done.38) | copy-start | bytes 6148
  453.4 138.2 %copy-start.41 = (f32[1,2,2,128]{3,1,2,0:T(2,128)S(1)}, f32[1,2,2,128]{3,1,2,0:T(2,128)}, u32[]{:S(2)}) copy-start(f32[1,2,2,128]{3,1,2,0:T(2,128)} %copy-done.40) | copy-start | bytes 6148
  453.4 226.6 %all-reduce.14.cloned.1.call-start = ((), (), s32[]{:S(2)}) async-start(), calls=%async_computation.17 | async-start | bytes 3538944 | tf_op jit(solution)/shard_map/psum | solution.py:276
  565.5 28.4 %copy-start.50 = (f32[768]{0:T(1024)S(1)}, f32[768]{0:T(1024)}, u32[]{:S(2)}) copy-start(f32[768]{0:T(1024)} %get-tuple-element.484) | copy-start | bytes 9220
  565.5 28.4 %copy-start.51 = (f32[768]{0:T(1024)S(1)}, f32[768]{0:T(1024)}, u32[]{:S(2)}) copy-start(f32[768]{0:T(1024)} %get-tuple-element.491) | copy-start | bytes 9220
  680.0 3.8 copy-start.25
  681.8 3.2 copy-start.24
  (33 other events, 61.0 us)
Sparse Core Ops, SparseCore 0:
  9.9 35.1 all-gather.4
  57.0 64.1 all-gather.6
  144.3 18.5 all-reduce.7
  164.6 38.5 all-gather.8
  204.8 37.3 all-gather.10
  250.6 20.3 all-reduce.9
  307.8 111.9 reduce-scatter.5
  423.2 25.8 reduce-scatter.9
  452.2 37.3 reduce-scatter.13
  492.5 37.3 reduce-scatter.11
  532.9 32.4 reduce-scatter.7
  568.2 23.3 all-reduce.11
  594.3 78.6 all-reduce.13
where the time goes:
time: 700 us; the launch traced here: 693 us
  waiting for transfers between devices  438 us (63%)
  blocking collectives  92.9 us (13%)
  matrix products  71.5 us (10%)
  other arithmetic  43.9 us (6%)
  local copies, waits for them, and re-layouts  25.2 us (4%)
  between operations  15 us (2%)
    reduce_scatter x4, waiting for transfers between devices, owned(): lax.psum_scatter(term.astype(jnp.bfloat16), 'fsdp', scatter_dimension=axi...  112 us
    reduce_scatter x1, waiting for transfers between devices, local(): lax.psum_scatter(pair_terms, 'ctx', scatter_dimension=1, tiled=True)  98 us
    psum x1, blocking collectives, local(): lax.psum((gain_one_grad, bias_one_grad, kernel_grad, shift_grad, gain_two...  81.9 us
    all_gather x1, waiting for transfers between devices, local(): whole_pairs = lax.all_gather(own_pairs, 'ctx', axis=1, tiled=True)  53.2 us
    all_gather x1, waiting for transfers between devices, local(): lax.all_gather(up_weight, 'fsdp', axis=0, tiled=True)  38.1 us
    all_gather x1, waiting for transfers between devices, local(): lax.all_gather(qkv_weight, 'fsdp', axis=0, tiled=True)  34.4 us
    all_gather x1, waiting for transfers between devices, local(): lax.all_gather(down_weight, 'fsdp', axis=1, tiled=True)  34.1 us
    psum x1, waiting for transfers between devices, local(): lax.psum(jnp.dot(act_low, down_full_w, preferred_element_type=jnp.float32...  26.1 us
  transfers between devices with their start and end apart: 15, of which 13 were waited for; matrix products, arithmetic and copies ran while one was open for 8% of the time, Pallas kernels for 0%

commit v1 on v0

--- a/solution.py
+++ b/solution.py
@@ -70,8 +70,22 @@
 ):
     batches, block_rows, model_width = tokens.shape
     all_rows = batches * block_rows
+
+    def raise_the_quarters(array_in):
+        devs = lax.axis_size("fsdp")
+        line_up = [(t, (t + 1) % devs) for t in range(devs)]
+        in_order = [(t, (t - 1) % devs) for t in range(devs)]
+        left_arr, back = ([array_in], [array_in])
+        for _ in range(devs // 2):
+            left_arr.append(lax.ppermute(left_arr[-1], "fsdp", line_up))
+        for _ in range((devs - 1) // 2):
+            back.append(lax.ppermute(back[-1], "fsdp", perm=in_order))
+        moved = jnp.concatenate([*left_arr[::-1], *back[1:]], 0)
+        arr_now = jnp.roll(moved, (lax.axis_index("fsdp") - devs // 2) * array_in.shape[0], axis=0)
+        return arr_now
+
     qkv_full, out_full, up_full_w, down_full_w = (
-        lax.all_gather(qkv_weight, "fsdp", axis=0, tiled=True),
+        raise_the_quarters(qkv_weight),
         lax.all_gather(out_weight, "fsdp", axis=1, tiled=True),
         lax.all_gather(up_weight, "fsdp", axis=0, tiled=True),
         lax.all_gather(down_weight, "fsdp", axis=1, tiled=True),

time: 700 us -> 678 us (0.969)
  waiting for transfers between devices: 438 us -> 405 us
    all_gather x1 -> x0, waiting for transfers between devices: 34.4 us -> none  [local(): lax.all_gather(qkv_weight, 'fsdp', axis=0, tiled=True)]
    ppermute x0 -> x3, waiting for transfers between devices: none -> 23.2 us  [the longest x2 23.2 us: raise_the_quarters(): left_arr.append(lax.ppermute(left_arr[-1], 'fsdp', line_up))]
    all_gather x1, waiting for transfers between devices: 38.1 us -> 16.9 us  [local(): lax.all_gather(up_weight, 'fsdp', axis=0, tiled=True)]
  transfers between devices with their start and end apart: 15 -> 17, of which waited for: 13 -> 14; matrix products, arithmetic and copies ran while one was open for 8% -> 8% of each run, Pallas kernels for 0% -> 0%
where the time goes in v1:
time: 678 us; the launch traced here: 670 us
  waiting for transfers between devices  405 us (60%)
  blocking collectives  93 us (14%)
  matrix products  69.9 us (10%)
  other arithmetic  47.1 us (7%)
  local copies, waits for them, and re-layouts  25.8 us (4%)
  between operations  16.7 us (2%)
  starting transfers between devices  11 us (2%)
    reduce_scatter x4, waiting for transfers between devices, owned(): lax.psum_scatter(term.astype(jnp.bfloat16), 'fsdp', scatter_dimension=axi...  112 us
    reduce_scatter x1, waiting for transfers between devices, local(): lax.psum_scatter(pair_terms, 'ctx', scatter_dimension=1, tiled=True)  98 us
    psum x1, blocking collectives, local(): lax.psum((gain_one_grad, bias_one_grad, kernel_grad, shift_grad, gain_two...  81.9 us
    all_gather x1, waiting for transfers between devices, local(): whole_pairs = lax.all_gather(own_pairs, 'ctx', axis=1, tiled=True)  53.4 us
    all_gather x1, waiting for transfers between devices, local(): lax.all_gather(down_weight, 'fsdp', axis=1, tiled=True)  34.2 us
    psum x1, waiting for transfers between devices, local(): lax.psum(jnp.dot(act_low, down_full_w, preferred_element_type=jnp.float32...  26.3 us
    ppermute x2, waiting for transfers between devices, raise_the_quarters(): left_arr.append(lax.ppermute(left_arr[-1], 'fsdp', line_up))  23.2 us
    psum x1, waiting for transfers between devices, local(): lax.psum(jnp.einsum('tf,df->td', up_grad_low, up_full_w, preferred_elemen...  20.3 us
  transfers between devices with their start and end apart: 17, of which 14 were waited for; matrix products, arithmetic and copies ran while one was open for 8% of the time, Pallas kernels for 0%

profile of v1, /device:TPU:0, one launch (start us, length us, event | category | flops | bytes accessed | tf_op | source)
XLA Modules:
  0.0 669.6 jit_solution(10560588730723999708)
XLA Ops:
  8.1 3.0 collective-permute-start
  15.0 8.3 %collective-permute-done = bf16[192,3,384]{2,0,1:T(8,128)(2,1)S(1)} collective-permute-done((bf16[192,3,384]{2,0,1:T(8,128)(2,1)}, bf16[192,3,384]{2,0,1:T(8,128)(2,1)S(1)}, u32[]{:S(2)}, u32[]{:S(2)}) %collective-permute-start) | collective-permute-done | bytes 442400 | tf_op jit(solution)/shard_map/ppermute | solution.py:80
  26.5 14.9 %collective-permute-done.1 = bf16[192,3,384]{2,0,1:T(8,128)(2,1)S(1)} collective-permute-done((bf16[192,3,384]{2,0,1:T(8,128)(2,1)S(1)}, bf16[192,3,384]{2,0,1:T(8,128)(2,1)S(1)}, u32[]{:S(2)}, u32[]{:S(2)}) %collective-permute-start.1) | collective-permute-done | bytes 442400 | tf_op jit(solution)/shard_map/ppermute | solution.py:80
  43.9 3.7 collective-permute-start.3
  50.1 2.1 add_convert_fusion
  53.2 11.1 %all_gather.13 = bf16[384,768]{0,1:T(8,128)(2,1)S(1)} all-gather(bf16[384,192]{0,1:T(8,128)(2,1)S(1)} %copy-done.27), channel_id=1, replica_groups=mesh['fsdp'=4,'ctx'=4,'tp'=2] {'fsdp'}, dimensions={1}, use_global_device_ids=true | all-gather | bytes 737280 | tf_op jit(solution)/shard_map/all_gather | solution.py:89
  64.4 53.4 %all-gather.4.cloned.1.call-done = bf16[2,1024,2,384]{1,3,0,2:T(8,128)(2,1)} async-done(((bf16[2,256,2,384]{1,3,0,2:T(8,128)(2,1)}), bf16[2,1024,2,384]{1,3,0,2:T(8,128)(2,1)}) %all-gather.4.cloned.1.call-update) | async-done | bytes 3145744 | tf_op jit(solution)/shard_map/all_gather | solution.py:125
  117.8 3.5 fusion.83
  121.3 6.7 while.48
  121.9 2.4 fusion.147
  124.3 3.6 exponential_reduce_fusion.2
  128.9 8.3 %while.49 = (s32[]{:T(128)}, f32[2,256,6,64]{1,3,2,0:T(8,128)}, s32[]{:T(128)}, s32[2]{0:T(128)S(1)}, bf16[2,256,6,64]{1,3,2,0:T(8,128)(2,1)S(1)}, /*index=5*/bf...) while((s32[]{:T(128)}, f32[2,256,6,64]{1,3,2,0:T(8,128)}, ...), condition=%wide.region_7.8_spmd.clone, body=%wide.region_6.7_spmd.clone.sunk | while | flops 818875648 | bytes 6715529 | solution.py:163
  129.7 7.6 %fusion.151 = f32[2,256,6,64]{1,3,2,0:T(8,128)} fusion(f32[2,256,6,64]{1,3,2,0:T(8,128)} %get-tuple-element.885, bf16[2,1024,6,64]{1,3,2,0:T(8,128)(2,1)} %get-tuple-element.902, f32[2,6,256]{2,1,0:T(8,128)S(1)} %bitcast.215, pred[2,256,1024]{2,1,0:T(8,128)(4,1)S(1)} %broadcast_and_fusion.9, bf16[2,256,6,64]{1,3,2,0:T(8,128)(2,1)S(1)} %get-tuple-element.899, ...), kind=kOutput, calls=%fused_computation.23.clone.1 | convolution fusion | flops 818085888 | bytes 5648384 | tf_op jit(solution)/shard_map/while/body/mhqk,mkhd->mqhd/dot_general | solution.py:156
  144.3 15.1 %all-reduce.8.cloned.1.call-done = f32[512,768]{1,0:T(8,128)} async-done(((f32[512,768]{1,0:T(8,128)}), f32[512,768]{1,0:T(8,128)}) %all-reduce.8.cloned.1.call-update) | async-done | bytes 1572880 | tf_op jit(solution)/shard_map/psum | solution.py:167
  161.6 16.9 %all-gather.6.cloned.1.call-done = bf16[768,1536]{1,0:T(8,128)(2,1)} async-done(((bf16[192,1536]{1,0:T(8,128)(2,1)}), bf16[768,1536]{1,0:T(8,128)(2,1)}) %all-gather.6.cloned.1.call-update) | async-done | bytes 2359312 | tf_op jit(solution)/shard_map/all_gather | solution.py:90
  178.5 4.8 convolution_maximum_fusion
  183.2 34.2 %all-gather.8.cloned.1.call-done = bf16[1536,768]{0,1:T(8,128)(2,1)} async-done(((bf16[1536,192]{0,1:T(8,128)(2,1)}), bf16[1536,768]{0,1:T(8,128)(2,1)}) %all-gather.8.cloned.1.call-update) | async-done | bytes 2359312 | tf_op jit(solution)/shard_map/all_gather | solution.py:91
  217.4 4.4 fusion.34
  223.0 2.6 fusion.87
  225.8 20.3 %all-reduce.10.cloned.1.call-done = f32[512,768]{1,0:T(8,128)} async-done(((f32[512,768]{1,0:T(8,128)}), f32[512,768]{1,0:T(8,128)}) %all-reduce.10.cloned.1.call-update) | async-done | bytes 1572880 | tf_op jit(solution)/shard_map/psum | solution.py:184
  246.1 2.9 multiply_reduce_fusion.4
  251.8 7.2 %while.50 = (s32[]{:T(128)}, f32[2,6,256,1]{2,0,1,3:T(2,128)S(1)}, s32[]{:T(128)}, s32[2]{0:T(128)S(1)}, bf16[2,256,6,64]{1,3,2,0:T(8,128)(2,1)S(1)}, /*index=5*...) while((s32[]{:T(128)}, f32[2,6,256,1]{2,0,1,3:T(2,128)S(1)}, ...), condition=%wide.region_17.18_spmd.clone, body=%wide.region_15.17_spmd.clone.sunk | while | flops 821824768 | bytes 37042348 | solution.py:211
  254.2 4.7 multiply_reduce_fusion.10
  259.8 3.4 broadcast_in_dim.65
  263.2 19.2 %while.51 = (s32[]{:T(128)}, f32[2,256,6,64]{1,3,2,0:T(8,128)S(1)}, f32[2,1024,2,384]{1,3,0,2:T(8,128)}, s32[]{:T(128)}, s32[2]{0:T(128)S(1)}, /*index=5*/bf16[2...) while((s32[]{:T(128)}, f32[2,256,6,64]{1,3,2,0:T(8,128)S(1)}, ...), condition=%wide.region_19.20_spmd.clone, body=%wide.region_18.19_spmd.clone.sunk | while | flops 2048265472 | bytes 87087288 | solution.py:257
  266.1 3.4 fusion.169
  269.5 6.5 multiply_convert_fusion.5
  276.0 2.1 fusion.168
  279.3 3.2 pad_maximum_fusion.5
  285.5 4.9 convolution_convert_fusion
  292.1 4.5 convolution_convert_fusion.1
  296.6 98.0 %reduce-scatter.6.cloned.1.call-done = f32[2,256,2,384]{1,3,0,2:T(8,128)} async-done(((f32[2,1024,2,384]{1,3,0,2:T(8,128)}), f32[2,256,2,384]{1,3,0,2:T(8,128)}) %reduce-scatter.6.cloned.1.call-update) | async-done | bytes 1572880 | tf_op jit(solution)/shard_map/reduce_scatter | solution.py:258
  394.6 2.2 fusion.66
  399.8 4.4 collective-permute-done.4
  405.6 2.2 pad_maximum_fusion.1
  408.9 4.5 multiply_reduce_fusion.3
  414.4 2.7 bitcast_convert_fusion
  417.2 5.4 fusion.75
  424.0 4.2 fusion.63
  428.4 35.8 %reduce-scatter.14.cloned.1.call-done = bf16[1536,192]{0,1:T(8,128)(2,1)} async-done(((bf16[1536,768]{0,1:T(8,128)(2,1)}), bf16[1536,192]{0,1:T(8,128)(2,1)}) %reduce-scatter.14.cloned.1.call-update) | async-done | bytes 589840 | tf_op jit(solution)/shard_map/reduce_scatter | solution.py:287
  464.2 40.4 %reduce-scatter.12.cloned.1.call-done = bf16[192,1536]{1,0:T(8,128)(2,1)} async-done(((bf16[768,1536]{1,0:T(8,128)(2,1)}), bf16[192,1536]{1,0:T(8,128)(2,1)}) %reduce-scatter.12.cloned.1.call-update) | async-done | bytes 589840 | tf_op jit(solution)/shard_map/reduce_scatter | solution.py:287
  504.6 35.5 %reduce-scatter.8.cloned.1.call-done = bf16[192,3,384]{2,0,1:T(8,128)(2,1)} async-done(((bf16[768,3,384]{2,0,1:T(8,128)(2,1)}), bf16[192,3,384]{2,0,1:T(8,128)(2,1)}) %reduce-scatter.8.cloned.1.call-update) | async-done | bytes 442384 | tf_op jit(solution)/shard_map/reduce_scatter | solution.py:287
  540.2 26.3 %all-reduce.12.cloned.1.call-done = (f32[512,768]{1,0:T(8,128)}, f32[512,768]{1,0:T(8,128)}) async-done(((f32[512,768]{1,0:T(8,128)}, f32[512,768]{1,0:T(8,128)}), (f32[512,768]{1,0:T(8,128)}, f32[512,768]{1,0:T(8,128)})) %all-reduce.12.cloned.1.call-update) | async-done | bytes 3145744 | tf_op jit(solution)/shard_map/psum | solution.py:174
  566.5 2.2 fusion.55
  568.7 81.9 %all-reduce = (f32[768]{0:T(1024)}, f32[768]{0:T(1024)}, f32[3,3,384]{2,1,0:T(4,128)}, f32[3,384]{1,0:T(4,128)}, f32[768]{0:T(1024)}, /*index=5*/f32[768]{0:T(1024)}) all-reduce(f32[768]{0:T(1024)S(1)} %get-tuple-element.486, f32[768]{0:T(1024)S(1)} %get-tuple-element.492, ...), channel_id=1, replica_groups=mesh['fsdp'=4,'ctx'=4,'tp'=2] {'fsdp','ctx'}, use_global_device_ids=true, to_apply=%region_25.26 | all-reduce | flops 7680 | bytes 61440 | tf_op jit(solution)/shard_map/psum | solution.py:296
  650.6 2.6 add_convert_fusion.1
  656.6 2.0 convert_element_type.115
  658.6 2.2 convert_element_type.119
  (241 shorter events, 52.4 us)
Async XLA Ops:
  8.0 33.5 %copy-start.19 = (bf16[192,3,384]{2,0,1:T(8,128)(2,1)S(1)}, bf16[192,3,384]{2,0,1:T(8,128)(2,1)}, u32[]{:S(2)}) copy-start(bf16[192,3,384]{2,0,1:T(8,128)(2,1)} %param.26) | copy-start | bytes 1327108
  8.0 109.8 %all-gather.4.cloned.1.call-start = ((), (), s32[]{:S(2)}) async-start(), calls=%async_computation.5 | async-start | bytes 3932160 | tf_op jit(solution)/shard_map/all_gather | solution.py:125
  8.1 15.2 %collective-permute-start = (bf16[192,3,384]{2,0,1:T(8,128)(2,1)}, bf16[192,3,384]{2,0,1:T(8,128)(2,1)S(1)}, u32[]{:S(2)}, u32[]{:S(2)}) collective-permute-start(bf16[192,3,384]{2,0,1:T(8,128)(2,1)} %param.26), channel_id=1, source_target_pairs={{0,8},{8,16},{16,24},{24,0},{1,9},{9,17},{17,25},{25,1},{2,10},{10... | collective-permute-start | bytes 1327112 | tf_op jit(solution)/shard_map/ppermute | solution.py:80
  11.1 30.5 %collective-permute-start.2 = (bf16[192,3,384]{2,0,1:T(8,128)(2,1)}, bf16[192,3,384]{2,0,1:T(8,128)(2,1)S(1)}, u32[]{:S(2)}, u32[]{:S(2)}) collective-permute-start(bf16[192,3,384]{2,0,1:T(8,128)(2,1)} %param.26), channel_id=1, source_target_pairs={{0,24},{8,0},{16,8},{24,16},{1,25},{9,1},{17,9},{25,17},{2,26},{10... | collective-permute-start | bytes 1327112 | tf_op jit(solution)/shard_map/ppermute | solution.py:82
  13.4 28.2 %copy-start.36 = (f32[1,2,2,128]{3,1,2,0:T(2,128)}, f32[1,2,2,128]{3,1,2,0:T(2,128)S(1)}, u32[]{:S(2)}) copy-start(f32[1,2,2,128]{3,1,2,0:T(2,128)S(1)} %copy.100) | copy-start | bytes 6148
  23.3 18.1 %collective-permute-start.1 = (bf16[192,3,384]{2,0,1:T(8,128)(2,1)S(1)}, bf16[192,3,384]{2,0,1:T(8,128)(2,1)S(1)}, u32[]{:S(2)}, u32[]{:S(2)}) collective-permute-start(bf16[192,3,384]{2,0,1:T(8,128)(2,1)S(1)} %collective-permute-done), channel_id=1, source_target_pairs={{0,8},{8,16},{16,24},{24,0},{1,9},{9,17},{17,25},{25,1},{2,10},{10... | collective-permute-start | bytes 1327112 | tf_op jit(solution)/shard_map/ppermute | solution.py:80
  24.9 16.8 %copy-start.38 = (f32[1,2,2,128]{3,1,2,0:T(2,128)}, f32[1,2,2,128]{3,1,2,0:T(2,128)S(1)}, u32[]{:S(2)}) copy-start(f32[1,2,2,128]{3,1,2,0:T(2,128)S(1)} %copy.101) | copy-start | bytes 6148
  42.0 5.5 copy-start.47
  43.9 5.0 collective-permute-start.3
  53.2 106.2 %all-reduce.8.cloned.1.call-start = ((), (), s32[]{:S(2)}) async-start(), calls=%async_computation.6 | async-start | bytes 3145728 | tf_op jit(solution)/shard_map/psum | solution.py:167
  64.3 74.6 %copy-start.13 = (bf16[384,768]{0,1:T(8,128)(2,1)}, bf16[384,768]{0,1:T(8,128)(2,1)S(1)}, u32[]{:S(2)}) copy-start(bf16[384,768]{0,1:T(8,128)(2,1)S(1)} %all_gather.13) | copy-start | bytes 1769476
  64.4 56.9 %copy-start.26 = (s32[2]{0:T(128)S(1)}, s32[2]{0:T(128)}, u32[]{:S(2)}) copy-start(s32[2]{0:T(128)} %param.22) | copy-start | bytes 28
  140.7 37.8 %all-gather.6.cloned.1.call-start = ((), (), s32[]{:S(2)}) async-start(), calls=%async_computation.7 | async-start | bytes 2949120 | tf_op jit(solution)/shard_map/all_gather | solution.py:90
  141.3 76.1 %all-gather.8.cloned.1.call-start = ((), (), s32[]{:S(2)}) async-start(), calls=%async_computation.8 | async-start | bytes 2949120 | tf_op jit(solution)/shard_map/all_gather | solution.py:91
  141.9 104.2 %all-reduce.10.cloned.1.call-start = ((), (), s32[]{:S(2)}) async-start(), calls=%async_computation.9 | async-start | bytes 3145728 | tf_op jit(solution)/shard_map/psum | solution.py:184
  144.3 34.1 %copy-start.52 = (f32[768]{0:T(1024)S(1)}, f32[768]{0:T(1024)}, u32[]{:S(2)}) copy-start(f32[768]{0:T(1024)} %param.30) | copy-start | bytes 9220
  161.2 87.7 %copy-start.2 = (f32[512,768]{1,0:T(8,128)}, f32[512,768]{1,0:T(8,128)S(1)}, u32[]{:S(2)}) copy-start(f32[512,768]{1,0:T(8,128)S(1)} %get-tuple-element.584) | copy-start | bytes 4718596
  161.3 87.7 %copy-start.40 = (f32[512]{0:T(512)}, f32[512]{0:T(512)S(1)}, u32[]{:S(2)}) copy-start(f32[512]{0:T(512)S(1)} %broadcast_multiply_fusion.4) | copy-start | bytes 6148
  161.6 87.4 %copy-start.45 = (f32[512]{0:T(512)}, f32[512]{0:T(512)S(1)}, u32[]{:S(2)}) copy-start(f32[512]{0:T(512)S(1)} %add_rsqrt_fusion) | copy-start | bytes 6148
  217.4 5.5 copy-start.59
  225.6 169.0 %reduce-scatter.6.cloned.1.call-start = ((), (), s32[]{:S(2)}) async-start(), calls=%async_computation.10 | async-start | bytes 7864320 | tf_op jit(solution)/shard_map/reduce_scatter | solution.py:258
  246.1 2.9 copy-start.12
  282.5 3.0 copy-start.22
  282.5 145.8 %reduce-scatter.10.cloned.1.call-start = ((), (), s32[]{:S(2)}) async-start(), calls=%async_computation.12 | async-start | bytes 737280 | tf_op jit(solution)/shard_map/reduce_scatter | solution.py:287
  285.4 178.8 %reduce-scatter.14.cloned.1.call-start = ((), (), s32[]{:S(2)}) async-start(), calls=%async_computation.14 | async-start | bytes 2949120 | tf_op jit(solution)/shard_map/reduce_scatter | solution.py:287
  290.4 214.2 %reduce-scatter.12.cloned.1.call-start = ((), (), s32[]{:S(2)}) async-start(), calls=%async_computation.13 | async-start | bytes 2949120 | tf_op jit(solution)/shard_map/reduce_scatter | solution.py:287
  296.6 243.5 %reduce-scatter.8.cloned.1.call-start = ((), (), s32[]{:S(2)}) async-start(), calls=%async_computation.11 | async-start | bytes 2211840 | tf_op jit(solution)/shard_map/reduce_scatter | solution.py:287
  398.5 5.7 collective-permute-start.4
  405.5 3.3 copy-start.8
  405.5 3.3 copy-start.29
  405.5 3.3 copy-start.31
  405.5 3.3 copy-start.33
  408.8 5.5 copy-start.4
  408.8 5.5 copy-start.35
  408.9 5.5 copy-start.55
  408.9 5.5 copy-start.57
  408.9 5.5 copy-start.58
  417.1 5.4 copy-start.16
  417.1 149.3 %all-reduce.12.cloned.1.call-start = ((), (), s32[]{:S(2)}) async-start(), calls=%async_computation.15 | async-start | bytes 6291456 | tf_op jit(solution)/shard_map/psum | solution.py:174
  428.2 112.0 %copy-start.42 = (f32[3,384]{1,0:T(4,128)S(1)}, f32[3,384]{1,0:T(4,128)}, u32[]{:S(2)}) copy-start(f32[3,384]{1,0:T(4,128)} %get-tuple-element.481) | copy-start | bytes 13828
  428.2 112.0 %copy-start.43 = (f32[3,384]{1,0:T(4,128)S(1)}, f32[3,384]{1,0:T(4,128)}, u32[]{:S(2)}) copy-start(f32[3,384]{1,0:T(4,128)} %get-tuple-element.482) | copy-start | bytes 13828
  428.2 112.0 %copy-start.44 = (f32[3,384]{1,0:T(4,128)S(1)}, f32[3,384]{1,0:T(4,128)}, u32[]{:S(2)}) copy-start(f32[3,384]{1,0:T(4,128)} %get-tuple-element.483) | copy-start | bytes 13828
  428.2 138.3 %copy-start.37 = (f32[1,2,2,128]{3,1,2,0:T(2,128)S(1)}, f32[1,2,2,128]{3,1,2,0:T(2,128)}, u32[]{:S(2)}) copy-start(f32[1,2,2,128]{3,1,2,0:T(2,128)} %copy-done.36) | copy-start | bytes 6148
  428.2 138.3 %copy-start.39 = (f32[1,2,2,128]{3,1,2,0:T(2,128)S(1)}, f32[1,2,2,128]{3,1,2,0:T(2,128)}, u32[]{:S(2)}) copy-start(f32[1,2,2,128]{3,1,2,0:T(2,128)} %copy-done.38) | copy-start | bytes 6148
  428.2 140.4 %copy-start.48 = (f32[768]{0:T(1024)S(1)}, f32[768]{0:T(1024)}, u32[]{:S(2)}) copy-start(f32[768]{0:T(1024)} %get-tuple-element.484) | copy-start | bytes 9220
  428.3 140.4 %copy-start.49 = (f32[768]{0:T(1024)S(1)}, f32[768]{0:T(1024)}, u32[]{:S(2)}) copy-start(f32[768]{0:T(1024)} %get-tuple-element.491) | copy-start | bytes 9220
  428.3 226.6 %all-reduce.14.cloned.1.call-start = ((), (), s32[]{:S(2)}) async-start(), calls=%async_computation.16 | async-start | bytes 3538944 | tf_op jit(solution)/shard_map/psum | solution.py:290
  654.9 5.9 copy-start.23
  (31 other events, 54.6 us)
Sparse Core Ops, SparseCore 0:
  53.3 64.4 all-gather.3
  140.8 18.5 all-reduce.7
  225.7 20.3 all-reduce.9
  282.6 111.9 reduce-scatter.5
  397.9 25.8 reduce-scatter.9
  426.7 37.3 reduce-scatter.13
  467.2 37.3 reduce-scatter.11
  507.6 32.4 reduce-scatter.7
  543.1 23.3 all-reduce.11
  569.0 78.6 all-reduce.13
Sparse Core Ops, SparseCore 1:
  143.0 35.4 all-gather.5
  180.2 37.2 all-gather.7
